TPU v7x, 32 devices: a whole 2x2x4 slice. The times are simulated.
32 devices in a mesh: grp: 2 (over y), row: 16 (over z, x, core).
Axes of the slice: x: 2, y: 2, z: 4, core: 2. Of those that a mesh axis runs over, the one named last changes fastest.
Arguments:
- diag_blocks: float32 [8192, 512], P('row'), may hold values from -0.6 to 2.6
- lower_coupling: float32 [8192, 64], P('row'), may hold values from -0.3125 to 0.3125
- upper_coupling: float32 [8192, 64], P('row'), may hold values from -0.3125 to 0.3125
- right_sides: float32 [8192, 1024], P('row', 'grp'), parts along dimension 1, may hold values from -108 to 108
Outputs:
- solution: float32 [8192, 1024], P('row', 'grp'), parts along dimension 1
- res_norms: float32 [8, 1024], P(None, 'grp'), parts along dimension 1
There are 2 independent parts, one for each index of `grp`. A program takes and returns all parts, laid end to end along the dimension named above; an argument that names none is the same for every part. Nothing has to cross between parts.
All inputs are finite; a program needn't handle non-finite values.
Results may differ from a plain program's by a relative error of at most 0.0001.
Values sent between devices are 32-bit elements; how exact they have to be, the bound alone decides.
A program may use at most 64 MiB of HBM per device.

v0:
```python
import functools

import jax
import jax.numpy as jnp
from jax import lax
from jax.experimental import pallas as pl
from jax.experimental.pallas import tpu as pltpu
from jax.sharding import PartitionSpec as P

SWEEPS = 8
LANES = 128


def split(value):
    high = value.astype(jnp.bfloat16)
    low = (value - high.astype(jnp.float32)).astype(jnp.bfloat16)
    return high, low


def dot(left, right):
    return jnp.dot(left, right, preferred_element_type=jnp.float32)


def kernel(
    n, d_hbm, l_hbm, u_hbm, b_hbm, x_out, norm_out,
    dv, lv, uv, xs, a_hi, a_lo, c_hi, c_lo, inv, acc, rhs, halo,
    send, recv, part, nears, fars, lates, load_sem, send_sem, recv_sem, psend, precv,
):
    me = lax.axis_index("row")
    rows, cols = xs.shape
    width = lv.shape[0]
    groups = cols // LANES
    has = (me > 0, me < n - 1)
    last = rows - width

    loads = [pltpu.make_async_copy(d_hbm, dv, load_sem.at[0]),
             pltpu.make_async_copy(b_hbm, xs, load_sem.at[1]),
             pltpu.make_async_copy(l_hbm, lv, load_sem.at[2]),
             pltpu.make_async_copy(u_hbm, uv, load_sem.at[3])]
    for load in loads:
        load.start()

    barrier = pltpu.get_barrier_semaphore()

    def greet(o, carry):
        pl.semaphore_signal(barrier, inc=1, device_id={"row": lax.rem(me + o, n)})
        return carry

    lax.fori_loop(1, n, greet, 0)

    for side in range(2):
        @pl.when(jnp.logical_not(has[side]))
        def _():
            recv[:, side] = jnp.zeros_like(recv[:, side])

    def copy(s, side, g):
        target = me + 1 if side == 0 else me - 1
        return pltpu.make_async_remote_copy(
            src_ref=send.at[s, side, g], dst_ref=recv.at[s, side, g],
            send_sem=send_sem.at[s, side, g], recv_sem=recv_sem.at[s, side, g],
            device_id={"row": target})

    def ship(s, g):
        for side in range(2):
            @pl.when(has[1 - side])
            def _():
                copy(s, side, g).start()

    def keep(r, top, g):
        size = r.shape[0]
        d = r * inv[top:top + size]
        high, low = split(d)
        rhs[top:top + size, :LANES] = high
        rhs[top:top + size, LANES:] = low
        return d, jnp.sum(r * r, axis=0, keepdims=True)

    def advance(g):
        both = dot(a_hi[...], rhs[...])
        acc[g] = both[:, :LANES] + both[:, LANES:] + dot(a_lo[...], rhs[:, :LANES])

    def span(g):
        return slice(g * LANES, (g + 1) * LANES)

    loads[0].wait()
    for m in range(rows // LANES):
        block = dv[m * LANES:(m + 1) * LANES, m * LANES:(m + 1) * LANES]
        eye = (lax.broadcasted_iota(jnp.int32, block.shape, 0)
               == lax.broadcasted_iota(jnp.int32, block.shape, 1))
        pivot = jnp.sum(jnp.where(eye, block, 0.0), axis=1, keepdims=True)
        inv[m * LANES:(m + 1) * LANES] = jnp.broadcast_to(1.0 / pivot, block.shape)
    loads[1].wait()
    for g in range(groups):
        send[0, 1, g] = xs[:width, span(g)] * inv[:width]
        send[0, 0, g] = xs[last:, span(g)] * inv[last:]
    pl.semaphore_wait(barrier, n - 1)
    for g in range(groups):
        ship(0, g)

    for m in range(rows // LANES):
        block = dv[m * LANES:(m + 1) * LANES]
        eye = (lax.broadcasted_iota(jnp.int32, block.shape, 0) + m * LANES
               == lax.broadcasted_iota(jnp.int32, block.shape, 1))
        a_hi[m * LANES:(m + 1) * LANES], a_lo[m * LANES:(m + 1) * LANES] = split(
            jnp.where(eye, 0.0, -block))
    loads[2].wait()
    loads[3].wait()
    c_hi[...], c_lo[...] = split(-jnp.concatenate([lv[...], uv[...]], axis=0).T)

    for g in range(groups):
        d, sums = keep(xs[:, span(g)], 0, g)
        part[0, g:g + 1] = sums
        xs[:, span(g)] = d
        advance(g)

    def sweep(s, final):
        for g in range(groups):
            for side in range(2):
                @pl.when(has[side])
                def _():
                    copy(s - 1, side, g).wait_recv()
            for side in range(2):
                high, low = split(recv[s - 1, side, g])
                halo[side * width:(side + 1) * width, :LANES] = high
                halo[side * width:(side + 1) * width, LANES:] = low

            def rest(top, size):
                both = dot(c_hi[top:top + size], halo[...])
                cross = dot(c_lo[top:top + size], halo[:, :LANES])
                return acc[g, top:top + size] + (both[:, :LANES] + both[:, LANES:] + cross)

            total = jnp.zeros((1, LANES), jnp.float32)
            for top, size in ((0, width), (last, width), (width, last - width)):
                d, sums = keep(rest(top, size), top, g)
                total = total + sums
                if size == width and not final:
                    send[s, 1 if top == 0 else 0, g] = d
                    if top == last:
                        ship(s, g)
                if final:
                    x_out[top:top + size, span(g)] = xs[top:top + size, span(g)] + d
                else:
                    xs[top:top + size, span(g)] += d
            part[s, g:g + 1] = total
            if not final:
                advance(g)

    def body(s, carry):
        sweep(s, False)
        return carry

    inner = nears.shape[0]
    outer = n // inner
    seat, bench = lax.rem(me, inner), lax.div(me, inner)
    done = SWEEPS - 1

    def near(o):
        return pltpu.make_async_remote_copy(
            src_ref=part.at[:done], dst_ref=nears.at[seat],
            send_sem=psend.at[0, o], recv_sem=precv.at[0, o],
            device_id={"row": bench * inner + lax.rem(seat + o, inner)})

    def far(o):
        return pltpu.make_async_remote_copy(
            src_ref=fars.at[bench], dst_ref=fars.at[bench],
            send_sem=psend.at[1, o], recv_sem=precv.at[1, o],
            device_id={"row": lax.rem(bench + o, outer) * inner + seat})

    def late(o):
        return pltpu.make_async_remote_copy(
            src_ref=part.at[done], dst_ref=lates.at[me],
            send_sem=psend.at[2, o], recv_sem=precv.at[2, o],
            device_id={"row": lax.rem(me + o, n)})

    def over(count, action):
        def one(o, carry):
            action(o)
            return carry

        lax.fori_loop(1, count, one, 0)

    lax.fori_loop(1, SWEEPS - 1, body, 0)
    over(inner, lambda o: near(o).start())
    nears[seat] = part[:done]
    sweep(SWEEPS - 1, True)
    over(n, lambda o: late(o).start())
    lates[me] = part[done]
    over(inner, lambda o: near(o).wait_recv())
    sums = nears[0]
    for j in range(1, inner):
        sums = sums + nears[j]
    fars[bench] = sums
    over(outer, lambda o: far(o).start())

    def drain(s, carry):
        for side in range(2):
            for g in range(groups):
                @pl.when(has[1 - side])
                def _():
                    copy(s, side, g).wait_send()
        return carry

    lax.fori_loop(0, SWEEPS - 1, drain, 0)
    over(inner, lambda o: near(o).wait_send())
    over(outer, lambda o: far(o).wait_recv())
    norms = fars[0]
    for j in range(1, outer):
        norms = norms + fars[j]
    norms = jnp.sqrt(norms)
    for s in range(done):
        for g in range(groups):
            norm_out[s:s + 1, span(g)] = norms[s, g:g + 1]
    over(n, lambda o: late(o).wait_recv())
    norm = jnp.sqrt(lax.fori_loop(1, n, lambda j, t: t + lates[j], lates[0]))
    for g in range(groups):
        norm_out[done:, span(g)] = norm[g:g + 1]
    over(outer, lambda o: far(o).wait_send())
    over(n, lambda o: late(o).wait_send())


def local(n, diag_blocks, lower_coupling, upper_coupling, right_sides):
    rows, cols = right_sides.shape
    width = lower_coupling.shape[1]
    groups = cols // LANES
    inner = max(a for a in range(1, n + 1) if n % a == 0 and a * a <= n)
    f32, bf16 = jnp.float32, jnp.bfloat16
    return pl.pallas_call(
        functools.partial(kernel, n),
        out_shape=(pltpu.VMEM((rows, cols), f32), pltpu.VMEM((SWEEPS, cols), f32)),
        in_specs=[pl.BlockSpec(memory_space=pltpu.HBM)] * 4,
        out_specs=[pl.BlockSpec(memory_space=pltpu.VMEM)] * 2,
        scratch_shapes=[
            pltpu.VMEM((rows, rows), f32),
            pltpu.VMEM((width, rows), f32),
            pltpu.VMEM((width, rows), f32),
            pltpu.VMEM((rows, cols), f32),
            pltpu.VMEM((rows, rows), bf16),
            pltpu.VMEM((rows, rows), bf16),
            pltpu.VMEM((rows, 2 * width), bf16),
            pltpu.VMEM((rows, 2 * width), bf16),
            pltpu.VMEM((rows, LANES), f32),
            pltpu.VMEM((groups, rows, LANES), f32),
            pltpu.VMEM((rows, 2 * LANES), bf16),
            pltpu.VMEM((2 * width, 2 * LANES), bf16),
            pltpu.VMEM((SWEEPS - 1, 2, groups, width, LANES), f32),
            pltpu.VMEM((SWEEPS - 1, 2, groups, width, LANES), f32),
            pltpu.VMEM((SWEEPS, groups, LANES), f32),
            pltpu.VMEM((inner, SWEEPS - 1, groups, LANES), f32),
            pltpu.VMEM((n // inner, SWEEPS - 1, groups, LANES), f32),
            pltpu.VMEM((n, groups, LANES), f32),
            pltpu.SemaphoreType.DMA((4,)),
            pltpu.SemaphoreType.DMA((SWEEPS - 1, 2, groups)),
            pltpu.SemaphoreType.DMA((SWEEPS - 1, 2, groups)),
            pltpu.SemaphoreType.DMA((3, n)),
            pltpu.SemaphoreType.DMA((3, n)),
        ],
        compiler_params=pltpu.CompilerParams(
            collective_id=0, has_side_effects=True, vmem_limit_bytes=62 * 2**20),
    )(diag_blocks, lower_coupling.T, upper_coupling.T, right_sides)


def solution(mesh):
    return jax.shard_map(
        functools.partial(local, mesh.shape["row"]),
        mesh=mesh,
        in_specs=(P("row", None), P("row", None), P("row", None), P("row", "grp")),
        out_specs=(P("row", "grp"), P(None, "grp")),
        check_vma=False,
    )
```

profile of v0, /device:TPU:0, one launch (start us, length us, event | category | flops | bytes accessed | tf_op | source)
XLA Modules:
  0.0 40.2 jit_solution(16305376595245394457)
XLA Ops:
  0.6 38.0 %shard_map.59 = (f32[512,512]{1,0:T(8,128)S(1)}, f32[8,512]{1,0:T(8,128)S(1)}) custom-call(f32[512,512]{1,0:T(8,128)} %d_hbm.1, f32[64,512]{1,0:T(8,128)} %bitcast.2, f32[64,512]{1,0:T(8,128)} %bitcast.3, f32[512,512]{1,0:T(8,128)} %b_hbm.1), custom_call_target="tpu_custom_call" | custom-call | tf_op jit(solution)/shard_map/pallas_call | solution.py:226
  38.7 1.0 %copy.8 = f32[512,512]{1,0:T(8,128)} copy(f32[512,512]{1,0:T(8,128)S(1)} %get-tuple-element.2) | data formatting | bytes 2097152
  39.6 0.6 %copy.9 = f32[8,512]{1,0:T(8,128)} copy(f32[8,512]{1,0:T(8,128)S(1)} %get-tuple-element.3) | data formatting | bytes 32768
where the time goes:
time: 40.4 us; the launch traced here: 40.2 us
  Pallas kernels  38 us (94%)
  local copies, waits for them, and re-layouts  1.58 us (4%)
  between operations  0.64 us (2%)
    pallas_call x1, Pallas kernels, local(): pl.pallas_call(functools.partial(kernel, n), out_shape=(pltpu.VMEM((rows,...  38 us
    unnamed x2, local copies, waits for them, and re-layouts  1.58 us

commit v1 on v0

v1 whole, which is shorter than its diff:
```python
import functools

import jax
import jax.numpy as jnp
from jax import lax
from jax.experimental import pallas as pl
from jax.experimental.pallas import tpu as pltpu
from jax.sharding import PartitionSpec as P

SWEEPS = 8
LANES = 128
GROUP = 256
STEP = 64


def split(value):
    high = value.astype(jnp.bfloat16)
    low = (value - high.astype(jnp.float32)).astype(jnp.bfloat16)
    return high, low


def dot(left, right):
    return jnp.dot(left, right, preferred_element_type=jnp.float32)


def halves(count):
    return pl.ds(0, count // 2), pl.ds(count // 2, count // 2)


def wide(column, size):
    return column if size == LANES else jnp.concatenate([column] * (size // LANES), axis=1)


def kernel(
    n, d_hbm, l_hbm, u_hbm, b_hbm, x_out, norm_out,
    dv, lu, xs, a_hi, a_lo, cf, c3, cx, w3, inv, acc, hi, lo, halo, own, pre, zs,
    send, recv, gsend, grecv, part, nears, fars, lates, load_sem, send_sem, recv_sem, gsem, psend, precv,
):
    me = lax.axis_index("row")
    rows, cols = xs.shape
    width = lu.shape[1]
    size = hi.shape[1]
    groups = cols // size
    last = rows - width
    chunks = rows // LANES
    core = lax.rem(me, 2)
    fast_row, slow_row = me + 1 - 2 * core, me - 1 + 2 * core
    has = jnp.logical_and(slow_row >= 0, slow_row < n)
    SLOW, FAST = 0, 1
    slow_rows = pl.ds(pl.multiple_of(core * last, width), width)
    fast_rows = pl.ds(pl.multiple_of((1 - core) * last, width), width)
    rest_rows = [pl.ds(pl.multiple_of(core * width + k * width, width), width) for k in range(last // width)]
    middle = pl.ds(width, last - width)

    order = [core * (chunks - 1), (1 - core) * (chunks - 1)] + list(range(1, chunks - 1))

    def chunk(m):
        return pl.ds(pl.multiple_of(m * LANES, LANES), LANES)

    def load(src, dst, k):
        return pltpu.make_async_copy(src, dst, load_sem.at[k])

    d_loads = [load(d_hbm.at[chunk(m)], dv.at[chunk(m)], k) for k, m in enumerate(order)]
    b_loads = [load(b_hbm.at[r], xs.at[r], chunks + k) for k, r in enumerate((slow_rows, fast_rows, middle))]
    c_loads = [load(l_hbm, lu.at[core], chunks + 3), load(u_hbm, lu.at[1 - core], chunks + 4)]
    for copy in (d_loads[0], b_loads[0], d_loads[1], b_loads[1], *c_loads, *d_loads[2:], b_loads[2]):
        copy.start()

    barrier = pltpu.get_barrier_semaphore()

    def greet(o, carry):
        pl.semaphore_signal(barrier, inc=1, device_id={"row": lax.rem(me + o, n)})
        return carry

    lax.fori_loop(1, n, greet, 0)

    @pl.when(jnp.logical_not(has))
    def _():
        recv[:, SLOW] = jnp.zeros_like(recv[:, SLOW])
        grecv[...] = jnp.zeros_like(grecv)

    def copy(s, side, g):
        return pltpu.make_async_remote_copy(
            src_ref=send.at[s, side, g], dst_ref=recv.at[s, side, g],
            send_sem=send_sem.at[s, side, g], recv_sem=recv_sem.at[s, side, g],
            device_id={"row": slow_row if side == SLOW else fast_row})

    reflect = pltpu.make_async_remote_copy(
        src_ref=gsend, dst_ref=grecv, send_sem=gsem.at[0], recv_sem=gsem.at[1],
        device_id={"row": slow_row})

    def ship(s, side, g):
        if side == FAST:
            copy(s, side, g).start()
        else:
            @pl.when(has)
            def _():
                copy(s, side, g).start()

    def span(g):
        return slice(g * size, (g + 1) * size)

    def scale(r):
        return wide(inv[r], size)

    def stack(ref, pair, *index):
        for k, value in enumerate((pair[0], pair[1], pair[0])):
            ref[*index, k * width:(k + 1) * width] = value

    def triple(value):
        high, low = split(value)
        return jnp.concatenate([high, high, low], axis=1)

    def keep(r, at, g, s):
        d = r * scale(at)
        hi[at], lo[at] = split(d)
        return d, jnp.sum(r * r, axis=0, keepdims=True)

    def note(s, g, sums):
        per = size // LANES
        for j in range(per):
            part[s, g * per + j:g * per + j + 1] = sums[:, j * LANES:(j + 1) * LANES]

    def advance(g):
        for at in halves(rows):
            acc[g, at] = dot(a_hi[at], hi[...]) + dot(a_hi[at], lo[...]) + dot(a_lo[at], hi[...])

    def pivots(m):
        block = dv[chunk(m), chunk(m)]
        eye = (lax.broadcasted_iota(jnp.int32, block.shape, 0)
               == lax.broadcasted_iota(jnp.int32, block.shape, 1))
        pivot = jnp.sum(jnp.where(eye, block, 0.0), axis=1, keepdims=True)
        inv[chunk(m)] = jnp.broadcast_to(1.0 / pivot, block.shape)

    def spread(m):
        for k in range(0, LANES, 32):
            at = pl.ds(pl.multiple_of(m * LANES + k, 32), 32)
            block = dv[at]
            eye = (lax.broadcasted_iota(jnp.int32, block.shape, 0) + (m * LANES + k)
                   == lax.broadcasted_iota(jnp.int32, block.shape, 1))
            a_hi[at], a_lo[at] = split(jnp.where(eye, 0.0, -block))

    d_loads[0].wait()
    pivots(order[0])
    b_loads[0].wait()
    for g in range(groups):
        send[0, SLOW, g] = xs[slow_rows, span(g)] * scale(slow_rows)
    d_loads[1].wait()
    pivots(order[1])
    b_loads[1].wait()
    for g in range(groups):
        send[0, FAST, g] = xs[fast_rows, span(g)] * scale(fast_rows)
    pl.semaphore_wait(barrier, n - 1)
    for g in range(groups):
        ship(0, FAST, g)
    ship(0, SLOW, 0)

    for c_load in c_loads:
        c_load.wait()
    cf[...] = -jnp.concatenate([lu[0], lu[1]], axis=0).T
    reflected = cf[slow_rows, :width] * inv[slow_rows, :width]
    gsend[...] = jnp.concatenate([reflected[:width // 2], reflected[width // 2:]], axis=1)

    @pl.when(has)
    def _():
        reflect.start()
    for g in range(1, groups):
        ship(0, SLOW, g)

    c3[...] = jnp.concatenate([triple(cf[:, width:]), triple(cf[:, :width])], axis=1)
    cx[...] = triple(cf[slow_rows, width:])
    for m in order[:2]:
        spread(m)
    for k, m in enumerate(order[2:]):
        d_loads[2 + k].wait()
        pivots(m)
        spread(m)

    b_loads[2].wait()
    for g in range(groups):
        total = jnp.zeros((1, size), jnp.float32)
        for k in range(0, rows, STEP):
            at = pl.ds(k, STEP)
            d, sums = keep(xs[at, span(g)], at, g, 0)
            total = total + sums
            xs[at, span(g)] = d
        note(0, g, total)
        stack(own, (hi[slow_rows], lo[slow_rows]), g)
        pre[g] = jnp.zeros_like(pre[g])
        advance(g)

    def early(s, g):
        copy(s, FAST, g).wait_recv()
        stack(halo, split(recv[s, FAST, g]), g, 0)

    def early_send(s, g):
        z = acc[g, slow_rows] + dot(cx[...], halo[g, 0].reshape(3 * width, size))
        send[s + 1, SLOW, g] = z * scale(slow_rows)
        ship(s + 1, SLOW, g)

    def correct(s, g, final):
        @pl.when(has)
        def _():
            copy(s, SLOW, g).wait_recv()
        stack(halo, split(recv[s, SLOW, g] + pre[g]), g, 1)
        total = jnp.zeros((1, size), jnp.float32)
        for at in halves(rows):
            zs[at] = dot(c3[at], halo[g].reshape(6 * width, size))
        for at in (fast_rows, *rest_rows):
            r = acc[g, at] + zs[at]
            if final:
                x_out[at, span(g)] = xs[at, span(g)] + r * scale(at)
                total = total + jnp.sum(r * r, axis=0, keepdims=True)
                continue
            d, sums = keep(r, at, g, s + 1)
            total = total + sums
            if at is fast_rows:
                send[s + 1, FAST, g] = d
                ship(s + 1, FAST, g)
            xs[at, span(g)] += d
        note(s + 1, g, total)

    def reflection(g):
        pre[g] = dot(w3[...], own[g])
        stack(own, (hi[slow_rows], lo[slow_rows]), g)

    early(0, 0)
    early_send(0, 0)

    def body(s, carry):
        for g in range(groups):
            correct(s, g, False)
            ahead = (s, g + 1) if g + 1 < groups else (s + 1, 0)
            early(*ahead)
            if g + 1 < groups:
                early_send(*ahead)
            else:
                @pl.when(s < SWEEPS - 3)
                def _():
                    early_send(*ahead)
            advance(g)
            if g == 0:
                @pl.when(s == 0)
                def _():
                    @pl.when(has)
                    def _():
                        reflect.wait_recv()
                    gathered = grecv[...]
                    w3[...] = triple(jnp.concatenate([gathered[:, :width], gathered[:, width:]], axis=0))
            reflection(g)
        return carry

    inner = nears.shape[0]
    outer = n // inner
    seat, bench = lax.rem(me, inner), lax.div(me, inner)
    done = SWEEPS - 1

    def near(o):
        return pltpu.make_async_remote_copy(
            src_ref=part.at[:done], dst_ref=nears.at[seat],
            send_sem=psend.at[0, o], recv_sem=precv.at[0, o],
            device_id={"row": bench * inner + lax.rem(seat + o, inner)})

    def far(o):
        return pltpu.make_async_remote_copy(
            src_ref=fars.at[bench], dst_ref=fars.at[bench],
            send_sem=psend.at[1, o], recv_sem=precv.at[1, o],
            device_id={"row": lax.rem(bench + o, outer) * inner + seat})

    def late(o):
        return pltpu.make_async_remote_copy(
            src_ref=part.at[done], dst_ref=lates.at[me],
            send_sem=psend.at[2, o], recv_sem=precv.at[2, o],
            device_id={"row": lax.rem(me + o, n)})

    def over(count, action):
        def one(o, carry):
            action(o)
            return carry

        lax.fori_loop(1, count, one, 0)

    lax.fori_loop(0, SWEEPS - 2, body, 0)
    over(inner, lambda o: near(o).start())
    nears[seat] = part[:done]
    for g in range(groups):
        correct(SWEEPS - 2, g, True)
        if g + 1 < groups:
            early(SWEEPS - 2, g + 1)
        if g == 0:
            over(inner, lambda o: near(o).wait_recv())
            sums = nears[0]
            for j in range(1, inner):
                sums = sums + nears[j]
            fars[bench] = sums
            over(outer, lambda o: far(o).start())
    over(n, lambda o: late(o).start())
    lates[me] = part[done]

    def drain(s, carry):
        for g in range(groups):
            copy(s, FAST, g).wait_send()

            @pl.when(has)
            def _():
                copy(s, SLOW, g).wait_send()
        return carry

    lax.fori_loop(0, SWEEPS - 1, drain, 0)

    @pl.when(has)
    def _():
        reflect.wait_send()
    over(inner, lambda o: near(o).wait_send())
    over(outer, lambda o: far(o).wait_recv())
    norms = fars[0]
    for j in range(1, outer):
        norms = norms + fars[j]
    norms = jnp.sqrt(norms)
    parts = cols // LANES
    for s in range(done):
        for g in range(parts):
            norm_out[s:s + 1, g * LANES:(g + 1) * LANES] = norms[s, g:g + 1]
    over(n, lambda o: late(o).wait_recv())
    norm = jnp.sqrt(lax.fori_loop(1, n, lambda j, t: t + lates[j], lates[0]))
    for g in range(parts):
        norm_out[done:, g * LANES:(g + 1) * LANES] = norm[g:g + 1]
    over(outer, lambda o: far(o).wait_send())
    over(n, lambda o: late(o).wait_send())


def local(n, diag_blocks, lower_coupling, upper_coupling, right_sides):
    rows, cols = right_sides.shape
    width = lower_coupling.shape[1]
    size = GROUP
    groups, parts = cols // size, cols // LANES
    inner = max(a for a in range(1, n + 1) if n % a == 0 and a * a <= n)
    f32, bf16 = jnp.float32, jnp.bfloat16
    return pl.pallas_call(
        functools.partial(kernel, n),
        out_shape=(pltpu.VMEM((rows, cols), f32), pltpu.VMEM((SWEEPS, cols), f32)),
        in_specs=[pl.BlockSpec(memory_space=pltpu.HBM)] * 4,
        out_specs=[pl.BlockSpec(memory_space=pltpu.VMEM)] * 2,
        scratch_shapes=[
            pltpu.VMEM((rows, rows), f32),
            pltpu.VMEM((2, width, rows), f32),
            pltpu.VMEM((rows, cols), f32),
            pltpu.VMEM((rows, rows), bf16),
            pltpu.VMEM((rows, rows), bf16),
            pltpu.VMEM((rows, 2 * width), f32),
            pltpu.VMEM((rows, 6 * width), bf16),
            pltpu.VMEM((width, 3 * width), bf16),
            pltpu.VMEM((width, 3 * width), bf16),
            pltpu.VMEM((rows, LANES), f32),
            pltpu.VMEM((groups, rows, size), f32),
            pltpu.VMEM((rows, size), bf16),
            pltpu.VMEM((rows, size), bf16),
            pltpu.VMEM((groups, 2, 3 * width, size), bf16),
            pltpu.VMEM((groups, 3 * width, size), bf16),
            pltpu.VMEM((groups, width, size), f32),
            pltpu.VMEM((rows, size), f32),
            pltpu.VMEM((SWEEPS - 1, 2, groups, width, size), f32),
            pltpu.VMEM((SWEEPS - 1, 2, groups, width, size), f32),
            pltpu.VMEM((width // 2, 2 * width), f32),
            pltpu.VMEM((width // 2, 2 * width), f32),
            pltpu.VMEM((SWEEPS, parts, LANES), f32),
            pltpu.VMEM((inner, SWEEPS - 1, parts, LANES), f32),
            pltpu.VMEM((n // inner, SWEEPS - 1, parts, LANES), f32),
            pltpu.VMEM((n, parts, LANES), f32),
            pltpu.SemaphoreType.DMA((rows // LANES + 5,)),
            pltpu.SemaphoreType.DMA((SWEEPS - 1, 2, groups)),
            pltpu.SemaphoreType.DMA((SWEEPS - 1, 2, groups)),
            pltpu.SemaphoreType.DMA((2,)),
            pltpu.SemaphoreType.DMA((3, n)),
            pltpu.SemaphoreType.DMA((3, n)),
        ],
        compiler_params=pltpu.CompilerParams(
            collective_id=0, has_side_effects=True, vmem_limit_bytes=62 * 2**20),
    )(diag_blocks, lower_coupling.T, upper_coupling.T, right_sides)


def solution(mesh):
    return jax.shard_map(
        functools.partial(local, mesh.shape["row"]),
        mesh=mesh,
        in_specs=(P("row", None), P("row", None), P("row", None), P("row", "grp")),
        out_specs=(P("row", "grp"), P(None, "grp")),
        check_vma=False,
    )
```

time: 40.4 us -> 38 us (0.941)
  Pallas kernels: 38 us -> 35.7 us
    pallas_call x1, Pallas kernels: 38 us -> 35.7 us  [local(): pl.pallas_call(functools.partial(kernel, n), out_shape=(pltpu.VMEM((rows,...]
where the time goes in v1:
time: 38 us; the launch traced here: 37.9 us
  Pallas kernels  35.7 us (94%)
  local copies, waits for them, and re-layouts  1.58 us (4%)
  between operations  0.64 us (2%)
    pallas_call x1, Pallas kernels, local(): pl.pallas_call(functools.partial(kernel, n), out_shape=(pltpu.VMEM((rows,...  35.7 us
    unnamed x2, local copies, waits for them, and re-layouts  1.58 us

profile of v1, /device:TPU:0, one launch (start us, length us, event | category | flops | bytes accessed | tf_op | source)
XLA Modules:
  0.0 37.9 jit_solution(18378914687176279130)
XLA Ops:
  0.6 35.7 %shard_map.59 = (f32[512,512]{1,0:T(8,128)S(1)}, f32[8,512]{1,0:T(8,128)S(1)}) custom-call(f32[512,512]{1,0:T(8,128)} %d_hbm.1, f32[64,512]{1,0:T(8,128)} %bitcast.2, f32[64,512]{1,0:T(8,128)} %bitcast.3, f32[512,512]{1,0:T(8,128)} %b_hbm.1), custom_call_target="tpu_custom_call" | custom-call | tf_op jit(solution)/shard_map/pallas_call | solution.py:339
  36.3 1.0 %copy.8 = f32[512,512]{1,0:T(8,128)} copy(f32[512,512]{1,0:T(8,128)S(1)} %get-tuple-element.2) | data formatting | bytes 2097152
  37.3 0.6 %copy.9 = f32[8,512]{1,0:T(8,128)} copy(f32[8,512]{1,0:T(8,128)S(1)} %get-tuple-element.3) | data formatting | bytes 32768

commit v2 on v1

--- a/solution.py
+++ b/solution.py
@@ -11,6 +11,7 @@
 LANES = 128
 GROUP = 256
 STEP = 64
+PAUSE = 3
 
 
 def split(value):
@@ -34,7 +35,7 @@
 def kernel(
     n, d_hbm, l_hbm, u_hbm, b_hbm, x_out, norm_out,
     dv, lu, xs, a_hi, a_lo, cf, c3, cx, w3, inv, acc, hi, lo, halo, own, pre, zs,
-    send, recv, gsend, grecv, part, nears, fars, lates, load_sem, send_sem, recv_sem, gsem, psend, precv,
+    send, recv, gsend, grecv, part, nears, fars, lates, load_sem, send_sem, recv_sem, gsem, psend, precv, lsem, waves,
 ):
     me = lax.axis_index("row")
     rows, cols = xs.shape
@@ -63,16 +64,29 @@
     d_loads = [load(d_hbm.at[chunk(m)], dv.at[chunk(m)], k) for k, m in enumerate(order)]
     b_loads = [load(b_hbm.at[r], xs.at[r], chunks + k) for k, r in enumerate((slow_rows, fast_rows, middle))]
     c_loads = [load(l_hbm, lu.at[core], chunks + 3), load(u_hbm, lu.at[1 - core], chunks + 4)]
-    for copy in (d_loads[0], b_loads[0], d_loads[1], b_loads[1], *c_loads, *d_loads[2:], b_loads[2]):
+    edge = pl.ds(pl.multiple_of(core * (rows - LANES), LANES), LANES)
+    for copy in (d_loads[0], b_loads[0], *c_loads, d_loads[1], b_loads[1], *d_loads[2:], b_loads[2]):
         copy.start()
 
     barrier = pltpu.get_barrier_semaphore()
 
-    def greet(o, carry):
-        pl.semaphore_signal(barrier, inc=1, device_id={"row": lax.rem(me + o, n)})
-        return carry
-
-    lax.fori_loop(1, n, greet, 0)
+    pl.semaphore_signal(barrier, inc=1, device_id={"row": fast_row})
+
+    @pl.when(has)
+    def _():
+        pl.semaphore_signal(barrier, inc=1, device_id={"row": slow_row})
+
+    reach = SWEEPS // 2
+    hops = [reach << k for k in range(n) if reach << k < n]
+
+    def wave(k):
+        for far_row in (me - hops[k], me + hops[k]):
+            @pl.when(jnp.logical_and(far_row >= 0, far_row < n))
+            def _():
+                pl.semaphore_signal(waves.at[k], inc=1, device_id={"row": far_row})
+
+    def await_wave(k):
+        pl.semaphore_wait(waves.at[k], (me >= hops[k]).astype(jnp.int32) + (me + hops[k] < n).astype(jnp.int32))
 
     @pl.when(jnp.logical_not(has))
     def _():
@@ -123,7 +137,10 @@
 
     def advance(g):
         for at in halves(rows):
-            acc[g, at] = dot(a_hi[at], hi[...]) + dot(a_hi[at], lo[...]) + dot(a_lo[at], hi[...])
+            total = jnp.zeros((rows // 2, size), jnp.float32)
+            for k in halves(rows):
+                total = total + (dot(a_hi[at, k], hi[k]) + dot(a_hi[at, k], lo[k]) + dot(a_lo[at, k], hi[k]))
+            acc[g, at] = total
 
     def pivots(m):
         block = dv[chunk(m), chunk(m)]
@@ -145,28 +162,21 @@
     b_loads[0].wait()
     for g in range(groups):
         send[0, SLOW, g] = xs[slow_rows, span(g)] * scale(slow_rows)
+    for c_load in c_loads:
+        c_load.wait()
+    cf[edge] = -jnp.concatenate([lu[0, :, edge], lu[1, :, edge]], axis=0).T
+    reflected = cf[slow_rows, :width] * inv[slow_rows, :width]
+    gsend[...] = jnp.concatenate([reflected[:width // 2], reflected[width // 2:]], axis=1)
+    pl.semaphore_wait(barrier, 1 + has.astype(jnp.int32))
+    ship(0, SLOW, 0)
     d_loads[1].wait()
     pivots(order[1])
     b_loads[1].wait()
     for g in range(groups):
         send[0, FAST, g] = xs[fast_rows, span(g)] * scale(fast_rows)
-    pl.semaphore_wait(barrier, n - 1)
-    for g in range(groups):
         ship(0, FAST, g)
-    ship(0, SLOW, 0)
-
-    for c_load in c_loads:
-        c_load.wait()
+
     cf[...] = -jnp.concatenate([lu[0], lu[1]], axis=0).T
-    reflected = cf[slow_rows, :width] * inv[slow_rows, :width]
-    gsend[...] = jnp.concatenate([reflected[:width // 2], reflected[width // 2:]], axis=1)
-
-    @pl.when(has)
-    def _():
-        reflect.start()
-    for g in range(1, groups):
-        ship(0, SLOW, g)
-
     c3[...] = jnp.concatenate([triple(cf[:, width:]), triple(cf[:, :width])], axis=1)
     cx[...] = triple(cf[slow_rows, width:])
     for m in order[:2]:
@@ -185,28 +195,41 @@
             total = total + sums
             xs[at, span(g)] = d
         note(0, g, total)
-        stack(own, (hi[slow_rows], lo[slow_rows]), g)
+        stack(own, (hi[slow_rows], lo[slow_rows]), g, 0)
         pre[g] = jnp.zeros_like(pre[g])
         advance(g)
-
-    def early(s, g):
+        if g + 1 < groups:
+            ship(0, SLOW, g + 1)
+
+    @pl.when(has)
+    def _():
+        reflect.start()
+
+    def share(g):
+        return dot(cx[...], halo[g, 0].reshape(3 * width, size))
+
+    def early(s, g, z):
+        send[s + 1, SLOW, g] = (acc[g, slow_rows] + z) * scale(slow_rows)
+
+        @pl.when(jnp.logical_and(has, s < SWEEPS - 2))
+        def _():
+            copy(s + 1, SLOW, g).start()
+
+    def take_fast(s, g):
         copy(s, FAST, g).wait_recv()
         stack(halo, split(recv[s, FAST, g]), g, 0)
 
-    def early_send(s, g):
-        z = acc[g, slow_rows] + dot(cx[...], halo[g, 0].reshape(3 * width, size))
-        send[s + 1, SLOW, g] = z * scale(slow_rows)
-        ship(s + 1, SLOW, g)
-
-    def correct(s, g, final):
+    def take_slow(s, g):
         @pl.when(has)
         def _():
             copy(s, SLOW, g).wait_recv()
         stack(halo, split(recv[s, SLOW, g] + pre[g]), g, 1)
+
+    def correct(s, g, final, between=lambda: None):
         total = jnp.zeros((1, size), jnp.float32)
-        for at in halves(rows):
-            zs[at] = dot(c3[at], halo[g].reshape(6 * width, size))
-        for at in (fast_rows, *rest_rows):
+        for k, at in enumerate((fast_rows, *rest_rows)):
+            if k == PAUSE:
+                between()
             r = acc[g, at] + zs[at]
             if final:
                 x_out[at, span(g)] = xs[at, span(g)] + r * scale(at)
@@ -220,40 +243,17 @@
             xs[at, span(g)] += d
         note(s + 1, g, total)
 
-    def reflection(g):
-        pre[g] = dot(w3[...], own[g])
-        stack(own, (hi[slow_rows], lo[slow_rows]), g)
-
-    early(0, 0)
-    early_send(0, 0)
-
-    def body(s, carry):
-        for g in range(groups):
-            correct(s, g, False)
-            ahead = (s, g + 1) if g + 1 < groups else (s + 1, 0)
-            early(*ahead)
-            if g + 1 < groups:
-                early_send(*ahead)
-            else:
-                @pl.when(s < SWEEPS - 3)
-                def _():
-                    early_send(*ahead)
-            advance(g)
-            if g == 0:
-                @pl.when(s == 0)
-                def _():
-                    @pl.when(has)
-                    def _():
-                        reflect.wait_recv()
-                    gathered = grecv[...]
-                    w3[...] = triple(jnp.concatenate([gathered[:, :width], gathered[:, width:]], axis=0))
-            reflection(g)
-        return carry
+    def couple(g):
+        for at in halves(rows):
+            zs[at] = dot(c3[at], halo[g].reshape(6 * width, size))
+
+    take_fast(0, 0)
+    early(0, 0, share(0))
 
     inner = nears.shape[0]
     outer = n // inner
     seat, bench = lax.rem(me, inner), lax.div(me, inner)
-    done = SWEEPS - 1
+    done = SWEEPS - 2
 
     def near(o):
         return pltpu.make_async_remote_copy(
@@ -269,9 +269,12 @@
 
     def late(o):
         return pltpu.make_async_remote_copy(
-            src_ref=part.at[done], dst_ref=lates.at[me],
-            send_sem=psend.at[2, o], recv_sem=precv.at[2, o],
+            src_ref=part.at[done:], dst_ref=lates.at[me],
+            send_sem=lsem.at[0], recv_sem=lsem.at[1],
             device_id={"row": lax.rem(me + o, n)})
+
+    def lates_all(k):
+        return pltpu.make_async_copy(lates.at[1:], lates.at[1:], lsem.at[k])
 
     def over(count, action):
         def one(o, carry):
@@ -280,22 +283,66 @@
 
         lax.fori_loop(1, count, one, 0)
 
-    lax.fori_loop(0, SWEEPS - 2, body, 0)
-    over(inner, lambda o: near(o).start())
+    def step(s, g, known):
+        ahead = (s, g + 1) if g + 1 < groups else (s + 1, 0)
+        take_slow(s, g)
+        take_fast(*ahead)
+        z = share(ahead[1])
+        couple(g)
+        if known:
+            pre[g] = dot(w3[...], own[g, 1])
+        early(*ahead, z)
+        correct(s, g, False)
+        advance(g)
+        stack(own, (hi[slow_rows], lo[slow_rows]), g, 1)
+
+    for g in range(groups):
+        step(0, g, False)
+
+    @pl.when(has)
+    def _():
+        reflect.wait_recv()
+    gathered = grecv[...]
+    w3[...] = triple(jnp.concatenate([gathered[:, :width], gathered[:, width:]], axis=0))
+    for g in range(groups):
+        pre[g] = dot(w3[...], own[g, 0])
+    def body(s, carry):
+        if hops:
+            @pl.when(s == reach - 1)
+            def _():
+                wave(0)
+
+        @pl.when(s == SWEEPS - 3)
+        def _():
+            if hops:
+                await_wave(0)
+            if len(hops) > 1:
+                wave(1)
+            over(inner, lambda o: near(o).start())
+        for g in range(groups):
+            step(s, g, True)
+        return carry
+
+    lax.fori_loop(1, SWEEPS - 2, body, 0)
+    for k in range(1, len(hops)):
+        await_wave(k)
+        if k + 1 < len(hops):
+            wave(k + 1)
     nears[seat] = part[:done]
-    for g in range(groups):
+    over(inner, lambda o: near(o).wait_recv())
+    sums = nears[0]
+    for j in range(1, inner):
+        sums = sums + nears[j]
+    fars[bench] = sums
+    over(outer, lambda o: far(o).start())
+    for g in range(groups):
+        take_slow(SWEEPS - 2, g)
+        if g + 1 < groups:
+            take_fast(SWEEPS - 2, g + 1)
+        couple(g)
         correct(SWEEPS - 2, g, True)
-        if g + 1 < groups:
-            early(SWEEPS - 2, g + 1)
-        if g == 0:
-            over(inner, lambda o: near(o).wait_recv())
-            sums = nears[0]
-            for j in range(1, inner):
-                sums = sums + nears[j]
-            fars[bench] = sums
-            over(outer, lambda o: far(o).start())
     over(n, lambda o: late(o).start())
-    lates[me] = part[done]
+    lates[me] = part[done:]
 
     def drain(s, carry):
         for g in range(groups):
@@ -313,20 +360,22 @@
         reflect.wait_send()
     over(inner, lambda o: near(o).wait_send())
     over(outer, lambda o: far(o).wait_recv())
-    norms = fars[0]
-    for j in range(1, outer):
-        norms = norms + fars[j]
-    norms = jnp.sqrt(norms)
     parts = cols // LANES
-    for s in range(done):
-        for g in range(parts):
-            norm_out[s:s + 1, g * LANES:(g + 1) * LANES] = norms[s, g:g + 1]
-    over(n, lambda o: late(o).wait_recv())
-    norm = jnp.sqrt(lax.fori_loop(1, n, lambda j, t: t + lates[j], lates[0]))
-    for g in range(parts):
-        norm_out[done:, g * LANES:(g + 1) * LANES] = norm[g:g + 1]
+
+    def finish(total, first):
+        norms = jnp.sqrt(total)
+        for s in range(total.shape[0]):
+            for g in range(parts):
+                norm_out[first + s:first + s + 1, g * LANES:(g + 1) * LANES] = norms[s, g:g + 1]
+
+    finish(sum((fars[j] for j in range(1, outer)), fars[0]), 0)
     over(outer, lambda o: far(o).wait_send())
-    over(n, lambda o: late(o).wait_send())
+    lates_all(0).wait()
+    lates_all(1).wait()
+    terms = [lates[j] for j in range(n)]
+    while len(terms) > 1:
+        terms = [a + b for a, b in zip(terms[::2], terms[1::2])] + terms[len(terms) // 2 * 2:]
+    finish(terms[0], done)
 
 
 def local(n, diag_blocks, lower_coupling, upper_coupling, right_sides):
@@ -356,23 +405,25 @@
             pltpu.VMEM((rows, size), bf16),
             pltpu.VMEM((rows, size), bf16),
             pltpu.VMEM((groups, 2, 3 * width, size), bf16),
-            pltpu.VMEM((groups, 3 * width, size), bf16),
+            pltpu.VMEM((groups, 2, 3 * width, size), bf16),
             pltpu.VMEM((groups, width, size), f32),
             pltpu.VMEM((rows, size), f32),
-            pltpu.VMEM((SWEEPS - 1, 2, groups, width, size), f32),
+            pltpu.VMEM((SWEEPS, 2, groups, width, size), f32),
             pltpu.VMEM((SWEEPS - 1, 2, groups, width, size), f32),
             pltpu.VMEM((width // 2, 2 * width), f32),
             pltpu.VMEM((width // 2, 2 * width), f32),
             pltpu.VMEM((SWEEPS, parts, LANES), f32),
-            pltpu.VMEM((inner, SWEEPS - 1, parts, LANES), f32),
-            pltpu.VMEM((n // inner, SWEEPS - 1, parts, LANES), f32),
-            pltpu.VMEM((n, parts, LANES), f32),
+            pltpu.VMEM((inner, SWEEPS - 2, parts, LANES), f32),
+            pltpu.VMEM((n // inner, SWEEPS - 2, parts, LANES), f32),
+            pltpu.VMEM((n, 2, parts, LANES), f32),
             pltpu.SemaphoreType.DMA((rows // LANES + 5,)),
             pltpu.SemaphoreType.DMA((SWEEPS - 1, 2, groups)),
             pltpu.SemaphoreType.DMA((SWEEPS - 1, 2, groups)),
             pltpu.SemaphoreType.DMA((2,)),
-            pltpu.SemaphoreType.DMA((3, n)),
-            pltpu.SemaphoreType.DMA((3, n)),
+            pltpu.SemaphoreType.DMA((2, n)),
+            pltpu.SemaphoreType.DMA((2, n)),
+            pltpu.SemaphoreType.DMA((2,)),
+            pltpu.SemaphoreType.REGULAR((max(n.bit_length() - 1, 1),)),
         ],
         compiler_params=pltpu.CompilerParams(
             collective_id=0, has_side_effects=True, vmem_limit_bytes=62 * 2**20),

time: 38 us -> 36 us (0.947)
  Pallas kernels: 35.7 us -> 33.6 us
    pallas_call x1, Pallas kernels: 35.7 us -> 33.6 us  [local(): pl.pallas_call(functools.partial(kernel, n), out_shape=(pltpu.VMEM((rows,...]
where the time goes in v2:
time: 36 us; the launch traced here: 35.8 us
  Pallas kernels  33.6 us (93%)
  local copies, waits for them, and re-layouts  1.58 us (4%)
  between operations  0.64 us (2%)
    pallas_call x1, Pallas kernels, local(): pl.pallas_call(functools.partial(kernel, n), out_shape=(pltpu.VMEM((rows,...  33.6 us
    unnamed x2, local copies, waits for them, and re-layouts  1.58 us

profile of v2, /device:TPU:0, one launch (start us, length us, event | category | flops | bytes accessed | tf_op | source)
XLA Modules:
  0.0 35.8 jit_solution(10738417505596188577)
XLA Ops:
  0.6 33.6 %shard_map.59 = (f32[512,512]{1,0:T(8,128)S(1)}, f32[8,512]{1,0:T(8,128)S(1)}) custom-call(f32[512,512]{1,0:T(8,128)} %d_hbm.1, f32[64,512]{1,0:T(8,128)} %bitcast.2, f32[64,512]{1,0:T(8,128)} %bitcast.3, f32[512,512]{1,0:T(8,128)} %b_hbm.1), custom_call_target="tpu_custom_call" | custom-call | tf_op jit(solution)/shard_map/pallas_call | solution.py:388
  34.3 1.0 %copy.8 = f32[512,512]{1,0:T(8,128)} copy(f32[512,512]{1,0:T(8,128)S(1)} %get-tuple-element.2) | data formatting | bytes 2097152
  35.2 0.6 %copy.9 = f32[8,512]{1,0:T(8,128)} copy(f32[8,512]{1,0:T(8,128)S(1)} %get-tuple-element.3) | data formatting | bytes 32768

commit v3 on v2

--- a/solution.py
+++ b/solution.py
@@ -22,6 +22,10 @@
 
 def dot(left, right):
     return jnp.dot(left, right, preferred_element_type=jnp.float32)
+
+
+def reaches(n):
+    return [hop for hop in (SWEEPS // 2 << k for k in range(n)) if hop < n]
 
 
 def halves(count):
@@ -76,8 +80,8 @@
     def _():
         pl.semaphore_signal(barrier, inc=1, device_id={"row": slow_row})
 
+    hops = reaches(n)
     reach = SWEEPS // 2
-    hops = [reach << k for k in range(n) if reach << k < n]
 
     def wave(k):
         for far_row in (me - hops[k], me + hops[k]):
@@ -96,7 +100,7 @@
     def copy(s, side, g):
         return pltpu.make_async_remote_copy(
             src_ref=send.at[s, side, g], dst_ref=recv.at[s, side, g],
-            send_sem=send_sem.at[s, side, g], recv_sem=recv_sem.at[s, side, g],
+            send_sem=send_sem.at[side], recv_sem=recv_sem.at[s, side, g],
             device_id={"row": slow_row if side == SLOW else fast_row})
 
     reflect = pltpu.make_async_remote_copy(
@@ -186,6 +190,8 @@
         pivots(m)
         spread(m)
 
+    for g in range(1, groups):
+        ship(0, SLOW, g)
     b_loads[2].wait()
     for g in range(groups):
         total = jnp.zeros((1, size), jnp.float32)
@@ -198,8 +204,6 @@
         stack(own, (hi[slow_rows], lo[slow_rows]), g, 0)
         pre[g] = jnp.zeros_like(pre[g])
         advance(g)
-        if g + 1 < groups:
-            ship(0, SLOW, g + 1)
 
     @pl.when(has)
     def _():
@@ -230,9 +234,8 @@
         for k, at in enumerate((fast_rows, *rest_rows)):
             if k == PAUSE:
                 between()
-            r = acc[g, at] + zs[at]
+            r = acc[g, at] + zs[g, at]
             if final:
-                x_out[at, span(g)] = xs[at, span(g)] + r * scale(at)
                 total = total + jnp.sum(r * r, axis=0, keepdims=True)
                 continue
             d, sums = keep(r, at, g, s + 1)
@@ -245,7 +248,7 @@
 
     def couple(g):
         for at in halves(rows):
-            zs[at] = dot(c3[at], halo[g].reshape(6 * width, size))
+            zs[g, at] = dot(c3[at], halo[g].reshape(6 * width, size))
 
     take_fast(0, 0)
     early(0, 0, share(0))
@@ -258,13 +261,13 @@
     def near(o):
         return pltpu.make_async_remote_copy(
             src_ref=part.at[:done], dst_ref=nears.at[seat],
-            send_sem=psend.at[0, o], recv_sem=precv.at[0, o],
+            send_sem=psend.at[0], recv_sem=precv.at[0],
             device_id={"row": bench * inner + lax.rem(seat + o, inner)})
 
     def far(o):
         return pltpu.make_async_remote_copy(
             src_ref=fars.at[bench], dst_ref=fars.at[bench],
-            send_sem=psend.at[1, o], recv_sem=precv.at[1, o],
+            send_sem=psend.at[1], recv_sem=precv.at[1],
             device_id={"row": lax.rem(bench + o, outer) * inner + seat})
 
     def late(o):
@@ -286,9 +289,9 @@
     def step(s, g, known):
         ahead = (s, g + 1) if g + 1 < groups else (s + 1, 0)
         take_slow(s, g)
+        couple(g)
         take_fast(*ahead)
         z = share(ahead[1])
-        couple(g)
         if known:
             pre[g] = dot(w3[...], own[g, 1])
         early(*ahead, z)
@@ -329,7 +332,8 @@
         if k + 1 < len(hops):
             wave(k + 1)
     nears[seat] = part[:done]
-    over(inner, lambda o: near(o).wait_recv())
+    if inner > 1:
+        pltpu.make_async_copy(nears.at[1:], nears.at[1:], precv.at[0]).wait()
     sums = nears[0]
     for j in range(1, inner):
         sums = sums + nears[j]
@@ -343,23 +347,25 @@
         correct(SWEEPS - 2, g, True)
     over(n, lambda o: late(o).start())
     lates[me] = part[done:]
-
-    def drain(s, carry):
-        for g in range(groups):
-            copy(s, FAST, g).wait_send()
-
-            @pl.when(has)
-            def _():
-                copy(s, SLOW, g).wait_send()
-        return carry
-
-    lax.fori_loop(0, SWEEPS - 1, drain, 0)
+    for g in range(groups):
+        for k in range(0, rows, STEP):
+            at = pl.ds(k, STEP)
+            x_out[at, span(g)] = xs[at, span(g)] + (acc[g, at] + zs[g, at]) * scale(at)
+
+    def sent(ref, sem):
+        return pltpu.make_async_copy(ref, ref, sem)
+
+    sent(recv.at[:, FAST], send_sem.at[FAST]).wait()
 
     @pl.when(has)
     def _():
+        sent(recv.at[:, SLOW], send_sem.at[SLOW]).wait()
         reflect.wait_send()
-    over(inner, lambda o: near(o).wait_send())
-    over(outer, lambda o: far(o).wait_recv())
+    if inner > 1:
+        sent(nears.at[1:], psend.at[0]).wait()
+    if outer > 1:
+        sent(fars.at[1:], psend.at[1]).wait()
+        sent(fars.at[1:], precv.at[1]).wait()
     parts = cols // LANES
 
     def finish(total, first):
@@ -369,7 +375,6 @@
                 norm_out[first + s:first + s + 1, g * LANES:(g + 1) * LANES] = norms[s, g:g + 1]
 
     finish(sum((fars[j] for j in range(1, outer)), fars[0]), 0)
-    over(outer, lambda o: far(o).wait_send())
     lates_all(0).wait()
     lates_all(1).wait()
     terms = [lates[j] for j in range(n)]
@@ -407,7 +412,7 @@
             pltpu.VMEM((groups, 2, 3 * width, size), bf16),
             pltpu.VMEM((groups, 2, 3 * width, size), bf16),
             pltpu.VMEM((groups, width, size), f32),
-            pltpu.VMEM((rows, size), f32),
+            pltpu.VMEM((groups, rows, size), f32),
             pltpu.VMEM((SWEEPS, 2, groups, width, size), f32),
             pltpu.VMEM((SWEEPS - 1, 2, groups, width, size), f32),
             pltpu.VMEM((width // 2, 2 * width), f32),
@@ -417,13 +422,13 @@
             pltpu.VMEM((n // inner, SWEEPS - 2, parts, LANES), f32),
             pltpu.VMEM((n, 2, parts, LANES), f32),
             pltpu.SemaphoreType.DMA((rows // LANES + 5,)),
-            pltpu.SemaphoreType.DMA((SWEEPS - 1, 2, groups)),
+            pltpu.SemaphoreType.DMA((2,)),
             pltpu.SemaphoreType.DMA((SWEEPS - 1, 2, groups)),
             pltpu.SemaphoreType.DMA((2,)),
-            pltpu.SemaphoreType.DMA((2, n)),
-            pltpu.SemaphoreType.DMA((2, n)),
             pltpu.SemaphoreType.DMA((2,)),
-            pltpu.SemaphoreType.REGULAR((max(n.bit_length() - 1, 1),)),
+            pltpu.SemaphoreType.DMA((2,)),
+            pltpu.SemaphoreType.DMA((2,)),
+            pltpu.SemaphoreType.REGULAR((max(len(reaches(n)), 1),)),
         ],
         compiler_params=pltpu.CompilerParams(
             collective_id=0, has_side_effects=True, vmem_limit_bytes=62 * 2**20),

time: 36 us -> 35.2 us (0.978)
  Pallas kernels: 33.6 us -> 32.8 us
    pallas_call x1, Pallas kernels: 33.6 us -> 32.8 us  [local(): pl.pallas_call(functools.partial(kernel, n), out_shape=(pltpu.VMEM((rows,...]
where the time goes in v3:
time: 35.2 us; the launch traced here: 35 us
  Pallas kernels  32.8 us (93%)
  local copies, waits for them, and re-layouts  1.58 us (4%)
  between operations  0.64 us (2%)
    pallas_call x1, Pallas kernels, local(): pl.pallas_call(functools.partial(kernel, n), out_shape=(pltpu.VMEM((rows,...  32.8 us
    unnamed x2, local copies, waits for them, and re-layouts  1.58 us

profile of v3, /device:TPU:0, one launch (start us, length us, event | category | flops | bytes accessed | tf_op | source)
XLA Modules:
  0.0 35.0 jit_solution(518597524842388250)
XLA Ops:
  0.6 32.8 %shard_map.59 = (f32[512,512]{1,0:T(8,128)S(1)}, f32[8,512]{1,0:T(8,128)S(1)}) custom-call(f32[512,512]{1,0:T(8,128)} %d_hbm.1, f32[64,512]{1,0:T(8,128)} %bitcast.2, f32[64,512]{1,0:T(8,128)} %bitcast.3, f32[512,512]{1,0:T(8,128)} %b_hbm.1), custom_call_target="tpu_custom_call" | custom-call | tf_op jit(solution)/shard_map/pallas_call | solution.py:393
  33.4 1.0 %copy.8 = f32[512,512]{1,0:T(8,128)} copy(f32[512,512]{1,0:T(8,128)S(1)} %get-tuple-element.2) | data formatting | bytes 2097152
  34.4 0.6 %copy.9 = f32[8,512]{1,0:T(8,128)} copy(f32[8,512]{1,0:T(8,128)S(1)} %get-tuple-element.3) | data formatting | bytes 32768

commit v4 on v3

--- a/solution.py
+++ b/solution.py
@@ -11,7 +11,7 @@
 LANES = 128
 GROUP = 256
 STEP = 64
-PAUSE = 3
+PAUSE = 2
 
 
 def split(value):
@@ -190,8 +190,6 @@
         pivots(m)
         spread(m)
 
-    for g in range(1, groups):
-        ship(0, SLOW, g)
     b_loads[2].wait()
     for g in range(groups):
         total = jnp.zeros((1, size), jnp.float32)
@@ -204,6 +202,8 @@
         stack(own, (hi[slow_rows], lo[slow_rows]), g, 0)
         pre[g] = jnp.zeros_like(pre[g])
         advance(g)
+        if g + 1 < groups:
+            ship(0, SLOW, g + 1)
 
     @pl.when(has)
     def _():
@@ -294,8 +294,7 @@
         z = share(ahead[1])
         if known:
             pre[g] = dot(w3[...], own[g, 1])
-        early(*ahead, z)
-        correct(s, g, False)
+        correct(s, g, False, lambda: early(*ahead, z))
         advance(g)
         stack(own, (hi[slow_rows], lo[slow_rows]), g, 1)
 
@@ -345,7 +344,8 @@
             take_fast(SWEEPS - 2, g + 1)
         couple(g)
         correct(SWEEPS - 2, g, True)
-    over(n, lambda o: late(o).start())
+    for o in range(1, n):
+        late(o).start()
     lates[me] = part[done:]
     for g in range(groups):
         for k in range(0, rows, STEP):

time: 35.2 us -> 34.7 us (0.986)
  Pallas kernels: 32.8 us -> 32.3 us
    pallas_call x1, Pallas kernels: 32.8 us -> 32.3 us  [local(): pl.pallas_call(functools.partial(kernel, n), out_shape=(pltpu.VMEM((rows,...]
where the time goes in v4:
time: 34.7 us; the launch traced here: 34.5 us
  Pallas kernels  32.3 us (93%)
  local copies, waits for them, and re-layouts  1.58 us (5%)
  between operations  0.64 us (2%)
    pallas_call x1, Pallas kernels, local(): pl.pallas_call(functools.partial(kernel, n), out_shape=(pltpu.VMEM((rows,...  32.3 us
    unnamed x2, local copies, waits for them, and re-layouts  1.58 us

profile of v4, /device:TPU:0, one launch (start us, length us, event | category | flops | bytes accessed | tf_op | source)
XLA Modules:
  0.0 34.5 jit_solution(16366602231769795225)
XLA Ops:
  0.6 32.3 %shard_map.59 = (f32[512,512]{1,0:T(8,128)S(1)}, f32[8,512]{1,0:T(8,128)S(1)}) custom-call(f32[512,512]{1,0:T(8,128)} %d_hbm.1, f32[64,512]{1,0:T(8,128)} %bitcast.2, f32[64,512]{1,0:T(8,128)} %bitcast.3, f32[512,512]{1,0:T(8,128)} %b_hbm.1), custom_call_target="tpu_custom_call" | custom-call | tf_op jit(solution)/shard_map/pallas_call | solution.py:393
  32.9 1.0 %copy.8 = f32[512,512]{1,0:T(8,128)} copy(f32[512,512]{1,0:T(8,128)S(1)} %get-tuple-element.2) | data formatting | bytes 2097152
  33.9 0.6 %copy.9 = f32[8,512]{1,0:T(8,128)} copy(f32[8,512]{1,0:T(8,128)S(1)} %get-tuple-element.3) | data formatting | bytes 32768

commit v5 on v4

--- a/solution.py
+++ b/solution.py
@@ -67,7 +67,7 @@
 
     d_loads = [load(d_hbm.at[chunk(m)], dv.at[chunk(m)], k) for k, m in enumerate(order)]
     b_loads = [load(b_hbm.at[r], xs.at[r], chunks + k) for k, r in enumerate((slow_rows, fast_rows, middle))]
-    c_loads = [load(l_hbm, lu.at[core], chunks + 3), load(u_hbm, lu.at[1 - core], chunks + 4)]
+    c_loads = [load(l_hbm, lu.at[core], chunks + 3), load(u_hbm, lu.at[1 - core], chunks + 3)]
     edge = pl.ds(pl.multiple_of(core * (rows - LANES), LANES), LANES)
     for copy in (d_loads[0], b_loads[0], *c_loads, d_loads[1], b_loads[1], *d_loads[2:], b_loads[2]):
         copy.start()
@@ -166,8 +166,7 @@
     b_loads[0].wait()
     for g in range(groups):
         send[0, SLOW, g] = xs[slow_rows, span(g)] * scale(slow_rows)
-    for c_load in c_loads:
-        c_load.wait()
+    load(lu, lu, chunks + 3).wait()
     cf[edge] = -jnp.concatenate([lu[0, :, edge], lu[1, :, edge]], axis=0).T
     reflected = cf[slow_rows, :width] * inv[slow_rows, :width]
     gsend[...] = jnp.concatenate([reflected[:width // 2], reflected[width // 2:]], axis=1)
@@ -421,7 +420,7 @@
             pltpu.VMEM((inner, SWEEPS - 2, parts, LANES), f32),
             pltpu.VMEM((n // inner, SWEEPS - 2, parts, LANES), f32),
             pltpu.VMEM((n, 2, parts, LANES), f32),
-            pltpu.SemaphoreType.DMA((rows // LANES + 5,)),
+            pltpu.SemaphoreType.DMA((rows // LANES + 4,)),
             pltpu.SemaphoreType.DMA((2,)),
             pltpu.SemaphoreType.DMA((SWEEPS - 1, 2, groups)),
             pltpu.SemaphoreType.DMA((2,)),

time: 34.7 us -> 34.7 us (level)
  no operation moved by 1% of the time
where the time goes in v5:
time: 34.7 us; the launch traced here: 34.5 us
  Pallas kernels  32.3 us (93%)
  local copies, waits for them, and re-layouts  1.58 us (5%)
  between operations  0.64 us (2%)
    pallas_call x1, Pallas kernels, local(): pl.pallas_call(functools.partial(kernel, n), out_shape=(pltpu.VMEM((rows,...  32.3 us
    unnamed x2, local copies, waits for them, and re-layouts  1.58 us

profile of v5, /device:TPU:0, one launch (start us, length us, event | category | flops | bytes accessed | tf_op | source)
XLA Modules:
  0.0 34.5 jit_solution(9656655297332011988)
XLA Ops:
  0.6 32.3 %shard_map.59 = (f32[512,512]{1,0:T(8,128)S(1)}, f32[8,512]{1,0:T(8,128)S(1)}) custom-call(f32[512,512]{1,0:T(8,128)} %d_hbm.1, f32[64,512]{1,0:T(8,128)} %bitcast.2, f32[64,512]{1,0:T(8,128)} %bitcast.3, f32[512,512]{1,0:T(8,128)} %b_hbm.1), custom_call_target="tpu_custom_call" | custom-call | tf_op jit(solution)/shard_map/pallas_call | solution.py:392
  32.9 1.0 %copy.8 = f32[512,512]{1,0:T(8,128)} copy(f32[512,512]{1,0:T(8,128)S(1)} %get-tuple-element.2) | data formatting | bytes 2097152
  33.9 0.6 %copy.9 = f32[8,512]{1,0:T(8,128)} copy(f32[8,512]{1,0:T(8,128)S(1)} %get-tuple-element.3) | data formatting | bytes 32768
